TPU v7x, 32 devices: a whole 2x2x4 slice. The times are simulated.
32 devices in a mesh: px: 4 (over y, x), py: 8 (over z, core).
Axes of the slice: x: 2, y: 2, z: 4, core: 2. Of those that a mesh axis runs over, the one named last changes fastest.
Arguments:
- base_cell: int32 [4, 8, 4096, 3], P('px', 'py'), may hold values from 0 to 255, as said below
- cell_offset: float32 [4, 8, 4096, 3], P('px', 'py'), may hold values from 0 to 1
- charges: float32 [4, 8, 4096], P('px', 'py'), may hold values from -4 to 4
- spacing: float32 [3], replicated, may hold values from 0.9 to 1.2
- ewald_beta: float32 [1], replicated, may hold values from 0.3 to 0.42
Outputs:
- forces: float32 [4, 8, 4096, 3], P('px', 'py')
- atom_energy: float32 [4, 8, 4096], P('px', 'py')
Inputs may be any that keep to these rules, and one draw needn't show every extreme that they name: base_cell[i, j, a, 0] lies in [i * 16, (i + 1) * 16), base_cell[i, j, a, 1] in [j * 16, (j + 1) * 16), base_cell[i, j, a, 2] in [0, 256); within these ranges cells are uniform.
All inputs are finite; a program needn't handle non-finite values.
Results may differ from a plain program's by a relative error of at most 0.0003.
Values sent between devices are 32-bit elements.
A program may use at most 64 MiB of HBM per device.

v0:
```python
import functools

import jax
import jax.numpy as jnp
import numpy as np
from jax import lax
from jax.experimental import pallas as pl
from jax.experimental.pallas import tpu as pltpu
from jax.sharding import PartitionSpec as P

CX = 16
CY = 16
NZ = 256
SPAN = CX + 3
RIM = 4
MAIN = SPAN * CY
ROWS = -(-(MAIN + SPAN * RIM) // 128) * 128
TILE = 512
VMEM_LIMIT = 60 * 1024 * 1024
NN = (((1,), (0,)), ((), ()))
NT = (((1,), (1,)), ((), ()))
TN = (((0,), (0,)), ((), ()))


def cas(positions, length):
    angles = 2.0 * np.pi / length * (np.outer(np.arange(length), positions) % length)
    return np.cos(angles) + np.sin(angles)


def halves(value):
    high = value.astype(jnp.bfloat16)
    return high, (value - high.astype(jnp.float32)).astype(jnp.bfloat16)


def constant_halves(table):
    table = np.asarray(table, np.float32)
    high = table.astype(jnp.bfloat16)
    return jnp.asarray(high), jnp.asarray((table - high.astype(np.float32)).astype(jnp.bfloat16))


def dot3(left, right, dims):
    def product(a, b):
        return lax.dot_general(a, b, dims, preferred_element_type=jnp.float32)

    return product(left[0], right[0]) + (product(left[0], right[1]) + product(left[1], right[0]))


def spline_values(t):
    rest = 1.0 - t
    square = t * t
    cube = square * t
    return (
        rest * rest * rest / 6.0,
        (3.0 * cube - 6.0 * square + 4.0) / 6.0,
        (-3.0 * cube + 3.0 * square + 3.0 * t + 1.0) / 6.0,
        cube / 6.0,
    )


def spline_slopes(t):
    rest = 1.0 - t
    square = t * t
    return (-0.5 * rest * rest, 1.5 * square - 2.0 * t, -1.5 * square + t + 0.5, 0.5 * square)


def pick(masks, weights):
    chosen = jnp.where(masks[3], weights[3], 0.0)
    for step in (2, 1, 0):
        chosen = jnp.where(masks[step], weights[step], chosen)
    return chosen


def masks_of(slots, start):
    steps = slots - start
    return [steps == step for step in range(4)]


def rows_iota(rows, width):
    return lax.broadcasted_iota(jnp.int32, (rows, width), 0)


class Stencil:
    def __init__(self, cells, offs, span):
        near_x = cells[0:1, span] - lax.axis_index("px") * CX
        near_y = cells[1:2, span] - lax.axis_index("py") * CY
        near_z = cells[2:3, span]
        width = near_x.shape[1]
        rim = rows_iota(ROWS - MAIN, width)
        self.x = masks_of(rows_iota(24, width), near_x)
        self.y = masks_of(rows_iota(CY, width), near_y)
        self.rim_x = masks_of(rim // RIM, near_x)
        self.rim_y = masks_of(CY + rim % RIM, near_y)
        steps = (rows_iota(NZ, width) - near_z) & (NZ - 1)
        self.z = [steps == step for step in range(4)]
        t = offs[:, span]
        self.values = [spline_values(t[d : d + 1]) for d in range(3)]
        self.slopes = [spline_slopes(t[d : d + 1]) for d in range(3)]


def spread_kernel(cells, offs, charge, tz_h, tz_l, out, grid):
    grid[...] = jnp.zeros_like(grid)

    @pl.loop(0, charge.shape[1] // TILE)
    def _(step):
        span = pl.ds(pl.multiple_of(step * TILE, TILE), TILE)
        near = Stencil(cells, offs, span)
        amount = charge[:, span]
        row_x = pick(near.x, [w * amount for w in near.values[0]])
        row_y = pick(near.y, near.values[1])
        rim = pick(near.rim_x, [w * amount for w in near.values[0]]) * pick(
            near.rim_y, near.values[1]
        )
        planes = jnp.concatenate([row_x[x : x + 1] * row_y for x in range(SPAN)] + [rim], axis=0)
        grid[...] += dot3(halves(planes), halves(pick(near.z, near.values[2])), NT)

    out[...] = dot3((tz_h[...], tz_l[...]), halves(grid[...]), NT)


def middle_kernel(
    pieces_x, pieces_y, got, spacing, beta, ty_h, ty_l, mx_h, mx_l, row1, row3, rowm, col2, colm,
    sent, turned, wide,
):
    slice_z = NZ // (pieces_x * pieces_y)
    chunk = pieces_x * slice_z
    total_x = CX * pieces_x
    total_y = CY * pieces_y

    def corners():
        for x in range(SPAN):
            for j in range(pieces_y):
                lanes = pl.ds(x * chunk, chunk)
                own = pl.ds(j * chunk, chunk)
                yield pl.ds(x * CY, CY), pl.ds(j * CY, CY), own, lanes
                yield pl.ds(MAIN + x * RIM, RIM), pl.ds(total_y + j * RIM, RIM), own, lanes

    turned[...] = got[...].T
    wide[...] = jnp.zeros_like(wide)
    for narrow_rows, wide_rows, own, lanes in corners():
        wide[wide_rows, lanes] = turned[narrow_rows, own]
    ty = (ty_h[...], ty_l[...])
    mx = (mx_h[...], mx_l[...])
    spectrum = dot3(halves(dot3(ty, halves(wide[...]), NN)), mx, NN)
    mine = lax.axis_index("py") * pieces_x + lax.axis_index("px")
    width = spectrum.shape[1]

    def spread_scalar(ref, place):
        return jnp.full((1, width), ref[place], jnp.float32)

    s0, s1, s2 = (spread_scalar(spacing, d) for d in range(3))
    b = spread_scalar(beta, 0)
    squares = row1[...] / (s0 * s0) + row3[pl.ds(mine, 1), :] / (s2 * s2)
    squares = squares + col2[...] * (1.0 / (s1 * s1))
    safe = jnp.where(squares > 0.0, squares, 1.0)
    volume = s0 * s1 * s2 * float(total_x * total_y * NZ)
    table = jnp.exp(safe * (-(np.pi**2) / (b * b))) / (safe * (np.pi * volume))
    table = table * (rowm[pl.ds(mine, 1), :] * colm[...])
    spectrum = spectrum * jnp.where(squares > 0.0, table, 0.0)
    wide[...] = dot3(ty, halves(dot3(halves(spectrum), mx, NT)), TN)
    turned[...] = jnp.zeros_like(turned)
    for narrow_rows, wide_rows, own, lanes in corners():
        turned[narrow_rows, own] = wide[wide_rows, lanes]
    sent[...] = turned[...].T


def gather_kernel(cells, offs, charge, spacing, got, tz_h, tz_l, out, win_h, win_l):
    window = dot3(halves(got[...].T), (tz_h[...], tz_l[...]), NN)
    win_h[...], win_l[...] = halves(window)

    @pl.loop(0, charge.shape[1] // TILE)
    def _(step):
        span = pl.ds(pl.multiple_of(step * TILE, TILE), TILE)
        near = Stencil(cells, offs, span)
        amount = charge[:, span]
        views = (win_h[...], win_l[...])
        level = dot3(views, halves(pick(near.z, near.values[2])), NN)
        tilt = dot3(views, halves(pick(near.z, near.slopes[2])), NN)
        row_x, tilt_x = pick(near.x, near.values[0]), pick(near.x, near.slopes[0])
        row_y, tilt_y = pick(near.y, near.values[1]), pick(near.y, near.slopes[1])

        def over_x(rows, field):
            total = rows[0:1] * field[0:CY]
            for x in range(1, SPAN):
                total = total + rows[x : x + 1] * field[x * CY : (x + 1) * CY]
            return total

        plain, along_x, along_z = over_x(row_x, level), over_x(tilt_x, level), over_x(row_x, tilt)
        rim_x, rim_tx = pick(near.rim_x, near.values[0]), pick(near.rim_x, near.slopes[0])
        rim_y, rim_ty = pick(near.rim_y, near.values[1]), pick(near.rim_y, near.slopes[1])
        rim_level, rim_tilt = level[MAIN:], tilt[MAIN:]

        def both(main, rim):
            return jnp.sum(main, axis=0, keepdims=True) + jnp.sum(rim, axis=0, keepdims=True)

        sampled = both(plain * row_y, rim_level * rim_x * rim_y)
        grads = (
            both(along_x * row_y, rim_level * rim_tx * rim_y),
            both(plain * tilt_y, rim_level * rim_x * rim_ty),
            both(along_z * row_y, rim_tilt * rim_x * rim_y),
        )
        for d in range(3):
            scale = jnp.full((1, TILE), spacing[d], jnp.float32)
            out[pl.ds(d, 1), span] = -amount * grads[d] / scale
        out[pl.ds(3, 1), span] = 0.5 * amount * sampled


def signed(length):
    index = np.arange(length)
    return np.where(2 * index < length, index, index - length)


def moduli(length):
    return 1.0 / ((2.0 + np.cos(2.0 * np.pi / length * np.arange(length))) / 3.0) ** 2


def middle_tables(pieces_x, pieces_y):
    pieces = pieces_x * pieces_y
    slice_z = NZ // pieces
    total_x, total_y = CX * pieces_x, CY * pieces_y
    rim = np.zeros((total_y, pieces_y, RIM))
    starts = CY * (np.arange(pieces_y) + 1)
    places = starts[:, None] + np.arange(RIM - 1)[None, :]
    rim[:, :, : RIM - 1] = cas(places.reshape(-1), total_y).reshape(total_y, pieces_y, RIM - 1)
    ty = np.concatenate([cas(np.arange(total_y), total_y), rim.reshape(total_y, -1)], axis=1)
    places = (np.arange(SPAN)[:, None] + CX * np.arange(pieces_x)[None, :]).reshape(-1)
    mx = np.kron(cas(places, total_x).T, np.eye(slice_z))
    depth = -(-mx.shape[0] // 128) * 128
    mx = np.concatenate([mx, np.zeros((depth - mx.shape[0], mx.shape[1]))], axis=0)
    row1 = np.repeat((signed(total_x) / total_x) ** 2, slice_z)[None, :]
    row3 = np.tile(((signed(NZ) / NZ) ** 2).reshape(pieces, slice_z), (1, total_x))
    rowm = np.tile(moduli(NZ).reshape(pieces, slice_z), (1, total_x))
    rowm = rowm * np.repeat(moduli(total_x), slice_z)[None, :]
    col2 = ((signed(total_y) / total_y) ** 2)[:, None]
    colm = moduli(total_y)[:, None]
    plain = tuple(jnp.asarray(t, jnp.float32) for t in (row1, row3, rowm, col2, colm))
    return constant_halves(ty) + constant_halves(mx) + plain


def in_vmem(count):
    return [pl.BlockSpec(memory_space=pltpu.VMEM)] * count


def local(base_cell, cell_offset, charges, spacing, ewald_beta):
    pieces_x = lax.axis_size("px")
    pieces_y = lax.axis_size("py")
    pieces = pieces_x * pieces_y
    cells = base_cell.reshape(-1, 3).T
    offs = cell_offset.reshape(-1, 3).T
    charge = charges.reshape(1, -1)
    tz = constant_halves(cas(np.arange(NZ), NZ))
    params = pltpu.CompilerParams(vmem_limit_bytes=VMEM_LIMIT)
    scalars = pl.BlockSpec(memory_space=pltpu.SMEM)

    def trade(tensor):
        blocks = tensor.reshape(pieces, NZ // pieces, ROWS)
        got = lax.all_to_all(blocks, ("py", "px"), split_axis=0, concat_axis=0, tiled=True)
        return got.reshape(NZ, ROWS)

    field = jax.ShapeDtypeStruct((NZ, ROWS), jnp.float32)
    spectrum = pl.pallas_call(
        spread_kernel,
        out_shape=field,
        in_specs=in_vmem(5),
        out_specs=pl.BlockSpec(memory_space=pltpu.VMEM),
        scratch_shapes=[pltpu.VMEM((ROWS, NZ), jnp.float32)],
        compiler_params=params,
        name="spread",
    )(cells, offs, charge, *tz)
    tables = middle_tables(pieces_x, pieces_y)
    spectrum = pl.pallas_call(
        functools.partial(middle_kernel, pieces_x, pieces_y),
        out_shape=field,
        in_specs=in_vmem(1) + [scalars, scalars] + in_vmem(len(tables)),
        out_specs=pl.BlockSpec(memory_space=pltpu.VMEM),
        scratch_shapes=[
            pltpu.VMEM((ROWS, NZ), jnp.float32),
            pltpu.VMEM((tables[0].shape[1], tables[2].shape[0]), jnp.float32),
        ],
        compiler_params=params,
        name="middle",
    )(trade(spectrum), spacing, ewald_beta, *tables)
    results = pl.pallas_call(
        gather_kernel,
        out_shape=jax.ShapeDtypeStruct((4, charge.shape[1]), jnp.float32),
        in_specs=in_vmem(3) + [scalars] + in_vmem(3),
        out_specs=pl.BlockSpec(memory_space=pltpu.VMEM),
        scratch_shapes=[pltpu.VMEM((ROWS, NZ), jnp.bfloat16)] * 2,
        compiler_params=params,
        name="gather",
    )(cells, offs, charge, spacing, trade(spectrum), *tz)
    return results[:3].T.reshape(base_cell.shape), results[3].reshape(charges.shape)


def solution(mesh):
    placed = (P("px", "py", None, None), P("px", "py", None, None), P("px", "py", None), P(), P())
    return jax.shard_map(
        local,
        mesh=mesh,
        in_specs=placed,
        out_specs=(P("px", "py", None, None), P("px", "py", None)),
        check_vma=False,
    )
```

profile of v0, /device:TPU:0, one launch (start us, length us, event | category | flops | bytes accessed | tf_op | source)
XLA Modules:
  0.0 70.3 jit_solution(1757710595644326196)
XLA Ops:
  0.6 0.0 copy-start.1
  0.6 1.5 %copy.23 = f32[1,1,4096,3]{2,3,1,0:T(4,128)} copy(f32[1,1,4096,3]{2,1,3,0:T(1,128)} %param.17) | data formatting | bytes 98304
  2.1 0.0 copy-done.1
  2.1 0.7 copy.24
  2.8 8.8 %spread.1 = f32[256,384]{1,0:T(8,128)} custom-call(s32[3,4096]{1,0:T(4,128)} %bitcast.27, f32[3,4096]{1,0:T(4,128)} %bitcast.25, f32[1,4096]{1,0:T(1,128)} %bitcast.29, bf16[256,256]{1,0:T(8,128)(2,1)} %constant.22.clone.tz_h, bf16[256,256]{1,0:T(8,128)(2,1)} %constant.23.clone.tz_l), custom_call_target="tpu_custom_call" | custom-call | tf_op jit(solution)/shard_map/spread/pallas_call | solution.py:259
  11.6 7.4 %all-to-all-start = ((f32[32,8,384]{2,1,0:T(8,128)}), f32[32,8,384]{2,1,0:T(8,128)S(1)}, u32[]{:S(2)}, u32[]{:S(2)}) async-start(f32[32,8,384]{2,1,0:T(8,128)} %bitcast.21), calls=%async_computation | async-start | bytes 786432 | tf_op jit(solution)/shard_map/all_to_all | solution.py:255
  19.6 12.9 %all-to-all-done = f32[32,8,384]{2,1,0:T(8,128)S(1)} async-done(((f32[32,8,384]{2,1,0:T(8,128)}), f32[32,8,384]{2,1,0:T(8,128)S(1)}, u32[]{:S(2)}, u32[]{:S(2)}) %all-to-all-start) | async-done | bytes 393248 | tf_op jit(solution)/shard_map/all_to_all | solution.py:255
  32.5 0.0 copy-start
  32.5 0.8 %copy-done = f32[32,8,384]{2,1,0:T(8,128)} copy-done((f32[32,8,384]{2,1,0:T(8,128)}, f32[32,8,384]{2,1,0:T(8,128)S(1)}, u32[]{:S(2)}) %copy-start) | copy-done | bytes 393240
  33.3 5.2 %middle.1 = f32[256,384]{1,0:T(8,128)} custom-call(f32[256,384]{1,0:T(8,128)} %bitcast.23, f32[3]{0:T(128)} %spacing.3, f32[1]{0:T(128)S(6)} %copy.25.beta, bf16[128,160]{1,0:T(8,128)(2,1)} %constant.29.clone.ty_h, bf16[128,160]{1,0:T(8,128)(2,1)} %constant.30.clone.ty_l, bf16[640,512]{1,0:T(8,128)(2,1)} %constant.31.clone.mx_h, ...), custom_call_target="tpu_custom_call" | custom-call | tf_op jit(solution)/shard_map/middle/pallas_call | solution.py:269
  38.4 16.9 %all_to_all.10 = f32[32,8,384]{2,1,0:T(8,128)} all-to-all(f32[32,8,384]{2,1,0:T(8,128)} %bitcast.24), channel_id=1, replica_groups=mesh['px'=4,'py'=8] {'py','px'}, dimensions={0} | all-to-all | bytes 786432 | tf_op jit(solution)/shard_map/all_to_all | solution.py:255
  55.3 12.0 %gather.1 = f32[4,4096]{1,0:T(4,128)} custom-call(s32[3,4096]{1,0:T(4,128)} %bitcast.28, f32[3,4096]{1,0:T(4,128)} %bitcast.26, f32[1,4096]{1,0:T(1,128)} %bitcast.30, f32[3]{0:T(128)} %spacing.3, f32[256,384]{1,0:T(8,128)} %bitcast.22, bf16[256,256]{1,0:T(8,128)(2,1)} %constant.22.clone.tz_h, bf16[256,256]{1,0:T(8,128)(2,1)} %constant.23.clone.tz_l), custom_call_target="tpu_custom_call" | custom-call | tf_op jit(solution)/shard_map/gather/pallas_call | solution.py:281
  67.3 0.8 %slice_bitcast_fusion = f32[1,1,4096,3]{2,3,1,0:T(4,128)S(1)} fusion(f32[4,4096]{1,0:T(4,128)} %gather.1), kind=kLoop, calls=%fused_computation | loop fusion | bytes 98304 | tf_op jit(solution)/shard_map/reshape | solution.py:290
  68.2 1.5 %slice_bitcast_fusion.1 = f32[1,1,4096]{2,1,0:T(1,128)} fusion(f32[4,4096]{1,0:T(4,128)} %gather.1), kind=kLoop, calls=%fused_computation.3 | loop fusion | bytes 32768 | tf_op jit(solution)/shard_map/reshape;squeeze | solution.py:290
  69.6 0.7 copy.18
Async XLA Ops:
  0.6 1.5 %copy-start.1 = (s32[1,1,4096,3]{2,1,3,0:T(1,128)S(1)}, s32[1,1,4096,3]{2,1,3,0:T(1,128)}, u32[]{:S(2)}) copy-start(s32[1,1,4096,3]{2,1,3,0:T(1,128)} %param.16) | copy-start | bytes 147460
  11.6 20.9 %all-to-all-start = ((f32[32,8,384]{2,1,0:T(8,128)}), f32[32,8,384]{2,1,0:T(8,128)S(1)}, u32[]{:S(2)}, u32[]{:S(2)}) async-start(f32[32,8,384]{2,1,0:T(8,128)} %bitcast.21), calls=%async_computation | async-start | bytes 786432 | tf_op jit(solution)/shard_map/all_to_all | solution.py:255
  32.5 0.8 %copy-start = (f32[32,8,384]{2,1,0:T(8,128)}, f32[32,8,384]{2,1,0:T(8,128)S(1)}, u32[]{:S(2)}) copy-start(f32[32,8,384]{2,1,0:T(8,128)S(1)} %all-to-all-done) | copy-start | bytes 1179652
where the time goes:
time: 70.8 us; the launch traced here: 70.3 us
  Pallas kernels  26 us (37%)
  blocking collectives  16.9 us (24%)
  waiting for transfers between devices  12.9 us (18%)
  starting transfers between devices  7.36 us (10%)
  local copies, waits for them, and re-layouts  5.85 us (8%)
  between operations  1.3 us (2%)
    all_to_all x1, blocking collectives, trade(): lax.all_to_all(blocks, ('py', 'px'), split_axis=0, concat_axis=0, tiled=T...  16.9 us
    all_to_all x1, waiting for transfers between devices, trade(): lax.all_to_all(blocks, ('py', 'px'), split_axis=0, concat_axis=0, tiled=T...  12.9 us
    pallas_call x1, Pallas kernels, local(): pl.pallas_call(gather_kernel, out_shape=jax.ShapeDtypeStruct((4, charge.s...  12 us
    pallas_call x1, Pallas kernels, local(): pl.pallas_call(spread_kernel, out_shape=field, in_specs=in_vmem(5), out_s...  8.82 us
    all_to_all x1, starting transfers between devices, trade(): lax.all_to_all(blocks, ('py', 'px'), split_axis=0, concat_axis=0, tiled=T...  7.36 us
    pallas_call x1, Pallas kernels, local(): pl.pallas_call(functools.partial(middle_kernel, pieces_x, pieces_y), out_...  5.15 us
    unnamed x7, local copies, waits for them, and re-layouts  3.55 us
    another operation x1, local copies, waits for them, and re-layouts, local(): results[3].reshape(charges.shape)  1.46 us
  transfers between devices with their start and end apart: 1, of which 1 were waited for; matrix products, arithmetic and copies ran while one was open for 0% of the time, Pallas kernels for 0%

commit v1 on v0

--- a/solution.py
+++ b/solution.py
@@ -81,9 +81,9 @@
 
 class Stencil:
     def __init__(self, cells, offs, span):
-        near_x = cells[0:1, span] - lax.axis_index("px") * CX
-        near_y = cells[1:2, span] - lax.axis_index("py") * CY
-        near_z = cells[2:3, span]
+        near_x = cells[0, :, span] - lax.axis_index("px") * CX
+        near_y = cells[1, :, span] - lax.axis_index("py") * CY
+        near_z = cells[2, :, span]
         width = near_x.shape[1]
         rim = rows_iota(ROWS - MAIN, width)
         self.x = masks_of(rows_iota(24, width), near_x)
@@ -92,12 +92,62 @@
         self.rim_y = masks_of(CY + rim % RIM, near_y)
         steps = (rows_iota(NZ, width) - near_z) & (NZ - 1)
         self.z = [steps == step for step in range(4)]
-        t = offs[:, span]
-        self.values = [spline_values(t[d : d + 1]) for d in range(3)]
-        self.slopes = [spline_slopes(t[d : d + 1]) for d in range(3)]
-
-
-def spread_kernel(cells, offs, charge, tz_h, tz_l, out, grid):
+        self.values = [spline_values(offs[d, :, span]) for d in range(3)]
+        self.slopes = [spline_slopes(offs[d, :, span]) for d in range(3)]
+
+
+def exchange(pieces_x, src, dst, send_sem, recv_sem):
+    pieces = src.shape[0]
+    mine = lax.axis_index("py") * pieces_x + lax.axis_index("px")
+
+    def copy(step):
+        peer = (mine + step) % pieces
+        return pltpu.make_async_remote_copy(
+            src_ref=src.at[peer],
+            dst_ref=dst.at[mine],
+            send_sem=send_sem.at[step],
+            recv_sem=recv_sem.at[step],
+            device_id=(peer % pieces_x, peer // pieces_x),
+            device_id_type=pl.DeviceIdType.MESH,
+        )
+
+    @pl.loop(1, pieces)
+    def _(step):
+        copy(step).start()
+
+    dst[mine] = src[mine]
+
+    @pl.loop(1, pieces)
+    def _(step):
+        copy(step).wait()
+
+
+def field_kernel(
+    pieces_x, pieces_y, cells, offs, charge, spacing, beta, tz_h, tz_l, ty_h, ty_l, mx_hbm_h,
+    mx_hbm_l, row1, row3, rowm, col2, colm, out, grid, wide, mx_h, mx_l, src, dst, back, home,
+    table_sem, send_sem, recv_sem,
+):
+    pieces = pieces_x * pieces_y
+    slice_z = NZ // pieces
+    mine = lax.axis_index("py") * pieces_x + lax.axis_index("px")
+    loads = [
+        pltpu.make_async_copy(mx_hbm_h, mx_h, table_sem.at[0]),
+        pltpu.make_async_copy(mx_hbm_l, mx_l, table_sem.at[1]),
+    ]
+    for load in loads:
+        load.start()
+    barrier = pltpu.get_barrier_semaphore()
+
+    @pl.loop(1, pieces)
+    def _(step):
+        peer = (mine + step) % pieces
+        pl.semaphore_signal(
+            barrier,
+            inc=1,
+            device_id=(peer % pieces_x, peer // pieces_x),
+            device_id_type=pl.DeviceIdType.MESH,
+        )
+
     grid[...] = jnp.zeros_like(grid)
 
     @pl.loop(0, charge.shape[1] // TILE)
@@ -113,14 +163,10 @@
         planes = jnp.concatenate([row_x[x : x + 1] * row_y for x in range(SPAN)] + [rim], axis=0)
         grid[...] += dot3(halves(planes), halves(pick(near.z, near.values[2])), NT)
 
-    out[...] = dot3((tz_h[...], tz_l[...]), halves(grid[...]), NT)
-
-
-def middle_kernel(
-    pieces_x, pieces_y, got, spacing, beta, ty_h, ty_l, mx_h, mx_l, row1, row3, rowm, col2, colm,
-    sent, turned, wide,
-):
-    slice_z = NZ // (pieces_x * pieces_y)
+    src[...] = dot3((tz_h[...], tz_l[...]), halves(grid[...]), NT).reshape(src.shape)
+    pl.semaphore_wait(barrier, pieces - 1)
+    exchange(pieces_x, src, dst, send_sem.at[0], recv_sem.at[0])
+
     chunk = pieces_x * slice_z
     total_x = CX * pieces_x
     total_y = CY * pieces_y
@@ -133,14 +179,16 @@
                 yield pl.ds(x * CY, CY), pl.ds(j * CY, CY), own, lanes
                 yield pl.ds(MAIN + x * RIM, RIM), pl.ds(total_y + j * RIM, RIM), own, lanes
 
-    turned[...] = got[...].T
+    turned = grid
+    turned[...] = dst[...].reshape(NZ, ROWS).T
     wide[...] = jnp.zeros_like(wide)
     for narrow_rows, wide_rows, own, lanes in corners():
         wide[wide_rows, lanes] = turned[narrow_rows, own]
     ty = (ty_h[...], ty_l[...])
+    for load in loads:
+        load.wait()
     mx = (mx_h[...], mx_l[...])
     spectrum = dot3(halves(dot3(ty, halves(wide[...]), NN)), mx, NN)
-    mine = lax.axis_index("py") * pieces_x + lax.axis_index("px")
     width = spectrum.shape[1]
 
     def spread_scalar(ref, place):
@@ -159,10 +207,12 @@
     turned[...] = jnp.zeros_like(turned)
     for narrow_rows, wide_rows, own, lanes in corners():
         turned[narrow_rows, own] = wide[wide_rows, lanes]
-    sent[...] = turned[...].T
-
-
-def gather_kernel(cells, offs, charge, spacing, got, tz_h, tz_l, out, win_h, win_l):
+    back[...] = turned[...].T.reshape(back.shape)
+    exchange(pieces_x, back, home, send_sem.at[1], recv_sem.at[1])
+    out[...] = home[...].reshape(NZ, ROWS)
+
+
+def gather_kernel(cells, offs, charge, spacing, got, tz_h, tz_l, forces, energy, win_h, win_l):
     window = dot3(halves(got[...].T), (tz_h[...], tz_l[...]), NN)
     win_h[...], win_l[...] = halves(window)
 
@@ -199,8 +249,8 @@
         )
         for d in range(3):
             scale = jnp.full((1, TILE), spacing[d], jnp.float32)
-            out[pl.ds(d, 1), span] = -amount * grads[d] / scale
-        out[pl.ds(3, 1), span] = 0.5 * amount * sampled
+            forces[d, :, span] = -amount * grads[d] / scale
+        energy[:, span] = 0.5 * amount * sampled
 
 
 def signed(length):
@@ -235,59 +285,57 @@
     return constant_halves(ty) + constant_halves(mx) + plain
 
 
-def in_vmem(count):
-    return [pl.BlockSpec(memory_space=pltpu.VMEM)] * count
-
-
 def local(base_cell, cell_offset, charges, spacing, ewald_beta):
     pieces_x = lax.axis_size("px")
     pieces_y = lax.axis_size("py")
     pieces = pieces_x * pieces_y
-    cells = base_cell.reshape(-1, 3).T
-    offs = cell_offset.reshape(-1, 3).T
     charge = charges.reshape(1, -1)
+    atoms = charge.shape[1]
+    cells = jnp.transpose(base_cell, (0, 3, 1, 2)).reshape(3, 1, atoms)
+    offs = jnp.transpose(cell_offset, (0, 3, 1, 2)).reshape(3, 1, atoms)
     tz = constant_halves(cas(np.arange(NZ), NZ))
-    params = pltpu.CompilerParams(vmem_limit_bytes=VMEM_LIMIT)
+    tables = middle_tables(pieces_x, pieces_y)
+    vmem = pl.BlockSpec(memory_space=pltpu.VMEM)
     scalars = pl.BlockSpec(memory_space=pltpu.SMEM)
-
-    def trade(tensor):
-        blocks = tensor.reshape(pieces, NZ // pieces, ROWS)
-        got = lax.all_to_all(blocks, ("py", "px"), split_axis=0, concat_axis=0, tiled=True)
-        return got.reshape(NZ, ROWS)
-
-    field = jax.ShapeDtypeStruct((NZ, ROWS), jnp.float32)
-    spectrum = pl.pallas_call(
-        spread_kernel,
-        out_shape=field,
-        in_specs=in_vmem(5),
-        out_specs=pl.BlockSpec(memory_space=pltpu.VMEM),
-        scratch_shapes=[pltpu.VMEM((ROWS, NZ), jnp.float32)],
-        compiler_params=params,
-        name="spread",
-    )(cells, offs, charge, *tz)
-    tables = middle_tables(pieces_x, pieces_y)
-    spectrum = pl.pallas_call(
-        functools.partial(middle_kernel, pieces_x, pieces_y),
-        out_shape=field,
-        in_specs=in_vmem(1) + [scalars, scalars] + in_vmem(len(tables)),
-        out_specs=pl.BlockSpec(memory_space=pltpu.VMEM),
+    anywhere = pl.BlockSpec(memory_space=pl.ANY)
+    blocks = pltpu.VMEM((pieces, NZ // pieces, ROWS), jnp.float32)
+    field = pl.pallas_call(
+        functools.partial(field_kernel, pieces_x, pieces_y),
+        out_shape=jax.ShapeDtypeStruct((NZ, ROWS), jnp.float32),
+        in_specs=[vmem] * 3 + [scalars] * 2 + [vmem] * 4 + [anywhere] * 2 + [vmem] * 5,
+        out_specs=vmem,
         scratch_shapes=[
             pltpu.VMEM((ROWS, NZ), jnp.float32),
             pltpu.VMEM((tables[0].shape[1], tables[2].shape[0]), jnp.float32),
+            pltpu.VMEM(tables[2].shape, jnp.bfloat16),
+            pltpu.VMEM(tables[2].shape, jnp.bfloat16),
+            blocks,
+            blocks,
+            blocks,
+            blocks,
+            pltpu.SemaphoreType.DMA((2,)),
+            pltpu.SemaphoreType.DMA((2, pieces)),
+            pltpu.SemaphoreType.DMA((2, pieces)),
         ],
-        compiler_params=params,
-        name="middle",
-    )(trade(spectrum), spacing, ewald_beta, *tables)
-    results = pl.pallas_call(
+        compiler_params=pltpu.CompilerParams(
+            vmem_limit_bytes=VMEM_LIMIT, collective_id=0, has_side_effects=True
+        ),
+        name="field",
+    )(cells, offs, charge, spacing, ewald_beta, *tz, *tables)
+    forces, energy = pl.pallas_call(
         gather_kernel,
-        out_shape=jax.ShapeDtypeStruct((4, charge.shape[1]), jnp.float32),
-        in_specs=in_vmem(3) + [scalars] + in_vmem(3),
-        out_specs=pl.BlockSpec(memory_space=pltpu.VMEM),
+        out_shape=(
+            jax.ShapeDtypeStruct((3, 1, atoms), jnp.float32),
+            jax.ShapeDtypeStruct((1, atoms), jnp.float32),
+        ),
+        in_specs=[vmem] * 3 + [scalars] + [vmem] * 3,
+        out_specs=(vmem, vmem),
         scratch_shapes=[pltpu.VMEM((ROWS, NZ), jnp.bfloat16)] * 2,
-        compiler_params=params,
+        compiler_params=pltpu.CompilerParams(vmem_limit_bytes=VMEM_LIMIT),
         name="gather",
-    )(cells, offs, charge, spacing, trade(spectrum), *tz)
-    return results[:3].T.reshape(base_cell.shape), results[3].reshape(charges.shape)
+    )(cells, offs, charge, spacing, field, *tz)
+    forces = jnp.transpose(forces.reshape(1, 3, 1, atoms), (0, 2, 3, 1))
+    return forces, energy.reshape(charges.shape)
 
 
 def solution(mesh):

time: 70.8 us -> 49 us (0.69)
  the two profiles are of different devices: /device:TPU:0 before, /device:TPU:27 now
where the time goes in v1:
time: 49 us; the launch traced here: 48.8 us
  Pallas kernels  47.6 us (97%)
  between operations  1.28 us (3%)
    pallas_call x1, Pallas kernels, local(): pl.pallas_call(functools.partial(field_kernel, pieces_x, pieces_y), out_s...  35.8 us
    pallas_call x1, Pallas kernels, local(): pl.pallas_call(gather_kernel, out_shape=(jax.ShapeDtypeStruct((3, 1, atom...  11.8 us

profile of v1, /device:TPU:27, one launch (start us, length us, event | category | flops | bytes accessed | tf_op | source)
XLA Modules:
  0.0 48.8 jit_solution(12405855642116040016)
XLA Ops:
  1.3 35.8 %field.1.got = f32[256,384]{1,0:T(8,128)} custom-call(s32[3,1,4096]{2,1,0:T(1,128)} %bitcast.11, f32[3,1,4096]{2,1,0:T(1,128)} %bitcast.13, f32[1,4096]{1,0:T(1,128)} %bitcast.15, f32[3]{0:T(128)} %spacing.3, f32[1]{0:T(128)S(6)} %copy.18.beta, bf16[256,256]{1,0:T(8,128)(2,1)} %constant.22.clone.tz_h, bf16[256,256]{1,0:T(8,128)(2,1)} %constant.23.clone.tz_l, ...), custom_call_target="tpu_custom_call" | custom-call | tf_op jit(solution)/shard_map/field/pallas_call | solution.py:302
  37.1 11.8 %gather.1 = (f32[3,1,4096]{2,1,0:T(1,128)}, f32[1,4096]{1,0:T(1,128)}) custom-call(s32[3,1,4096]{2,1,0:T(1,128)} %bitcast.12, f32[3,1,4096]{2,1,0:T(1,128)} %bitcast.14, f32[1,4096]{1,0:T(1,128)} %bitcast.16, f32[3]{0:T(128)} %spacing.3, f32[256,384]{1,0:T(8,128)} %field.1.got, bf16[256,256]{1,0:T(8,128)(2,1)} %constant.22.clone.tz_h, ...), custom_call_target="tpu_custom_call" | custom-call | tf_op jit(solution)/shard_map/gather/pallas_call | solution.py:325

commit v2 on v1

v2 whole, which is shorter than its diff:
```python
import functools

import jax
import jax.numpy as jnp
import numpy as np
from jax import lax
from jax.experimental import pallas as pl
from jax.experimental.pallas import tpu as pltpu
from jax.sharding import PartitionSpec as P

CX = 16
CY = 16
NZ = 256
SPAN = CX + 3
RIM = 4
MAIN = SPAN * CY
CORE = CX * CY
ROWS = -(-(MAIN + SPAN * RIM) // 128) * 128
TILE = 512
VMEM_LIMIT = 60 * 1024 * 1024
NN = (((1,), (0,)), ((), ()))
NT = (((1,), (1,)), ((), ()))
TN = (((0,), (0,)), ((), ()))


def cas(positions, length):
    angles = 2.0 * np.pi / length * (np.outer(np.arange(length), positions) % length)
    return np.cos(angles) + np.sin(angles)


def halves(value):
    high = value.astype(jnp.bfloat16)
    return high, (value - high.astype(jnp.float32)).astype(jnp.bfloat16)


def constant_halves(table):
    table = np.asarray(table, np.float32)
    high = table.astype(jnp.bfloat16)
    return jnp.asarray(high), jnp.asarray((table - high.astype(np.float32)).astype(jnp.bfloat16))


def dot3(left, right, dims):
    def product(a, b):
        return lax.dot_general(a, b, dims, preferred_element_type=jnp.float32)

    if dims == TN:
        cross = product(left[0], right[1]) + product(left[1], right[0])
        return product(left[0], right[0]) + cross
    rows = left[0].shape[0]
    stacked = product(jnp.concatenate(left, axis=0), right[0])
    return stacked[:rows] + (stacked[rows:] + product(left[0], right[1]))


def spline_values(t):
    rest = 1.0 - t
    square = t * t
    cube = square * t
    return (
        rest * rest * rest / 6.0,
        (3.0 * cube - 6.0 * square + 4.0) / 6.0,
        (-3.0 * cube + 3.0 * square + 3.0 * t + 1.0) / 6.0,
        cube / 6.0,
    )


def spline_slopes(t):
    rest = 1.0 - t
    square = t * t
    return (-0.5 * rest * rest, 1.5 * square - 2.0 * t, -1.5 * square + t + 0.5, 0.5 * square)


def pick(masks, weights):
    chosen = jnp.where(masks[3], weights[3], 0.0)
    for step in (2, 1, 0):
        chosen = jnp.where(masks[step], weights[step], chosen)
    return chosen


def masks_of(slots, start):
    steps = slots - start
    return [steps == step for step in range(4)]


def rows_iota(rows, width):
    return lax.broadcasted_iota(jnp.int32, (rows, width), 0)


class Stencil:
    def __init__(self, cells, offs, span):
        self.near_x = cells[0, :, span] - lax.axis_index("px") * CX
        self.near_y = cells[1, :, span] - lax.axis_index("py") * CY
        self.near_z = cells[2, :, span]
        self.width = self.near_x.shape[1]
        self.t = [offs[d, :, span] for d in range(3)]

    def x(self):
        return masks_of(rows_iota(24, self.width), self.near_x)

    def y(self):
        return masks_of(rows_iota(CY, self.width), self.near_y)

    def rim(self):
        rim = rows_iota(ROWS - MAIN, self.width)
        return masks_of(rim // RIM, self.near_x), masks_of(CY + rim % RIM, self.near_y)

    def z(self):
        steps = (rows_iota(NZ, self.width) - self.near_z) & (NZ - 1)
        return [steps == step for step in range(4)]

    def values(self, d):
        return spline_values(self.t[d])

    def slopes(self, d):
        return spline_slopes(self.t[d])


class Exchange:
    def __init__(self, pieces_x, src, dst, lanes, send_sem, recv_sem):
        self.pieces_x, self.src, self.dst, self.lanes = pieces_x, src, dst, lanes
        self.send_sem, self.recv_sem = send_sem, recv_sem
        self.pieces = src.shape[0]
        self.mine = lax.axis_index("py") * pieces_x + lax.axis_index("px")

    def copy(self, step):
        peer = (self.mine + step) % self.pieces
        return pltpu.make_async_remote_copy(
            src_ref=self.src.at[peer, :, self.lanes],
            dst_ref=self.dst.at[self.mine, :, self.lanes],
            send_sem=self.send_sem.at[step],
            recv_sem=self.recv_sem.at[step],
            device_id=(peer % self.pieces_x, peer // self.pieces_x),
            device_id_type=pl.DeviceIdType.MESH,
        )

    def put(self, value):
        self.src[:, :, self.lanes] = value.reshape(self.src.shape[:2] + (value.shape[1],))

        @pl.loop(1, self.pieces)
        def _(step):
            self.copy(step).start()

        self.dst[self.mine, :, self.lanes] = self.src[self.mine, :, self.lanes]

    def get(self):
        @pl.loop(1, self.pieces)
        def _(step):
            self.copy(step).wait()

        return self.dst[:, :, self.lanes].reshape(NZ, -1)


def kernel(
    pieces_x, pieces_y, cells, offs, charge, spacing, beta, tz_h, tz_l, ty_h, ty_l, mx_hbm_h,
    mx_hbm_l, row1, row3, rowm, col2, colm, forces, energy, grid, wide, mx_h, mx_l, rz_h, rz_l,
    dz_h, dz_l, window, part, src, dst, back, home, table_sem, send_sem, recv_sem,
):
    pieces = pieces_x * pieces_y
    slice_z = NZ // pieces
    mine = lax.axis_index("py") * pieces_x + lax.axis_index("px")
    core, edge = pl.ds(0, CORE), pl.ds(CORE, ROWS - CORE)
    loads = [
        pltpu.make_async_copy(mx_hbm_h, mx_h, table_sem.at[0]),
        pltpu.make_async_copy(mx_hbm_l, mx_l, table_sem.at[1]),
    ]
    for load in loads:
        load.start()
    barrier = pltpu.get_barrier_semaphore()

    @pl.loop(1, pieces)
    def _(step):
        peer = (mine + step) % pieces
        pl.semaphore_signal(
            barrier,
            inc=1,
            device_id=(peer % pieces_x, peer // pieces_x),
            device_id_type=pl.DeviceIdType.MESH,
        )

    def tiles(body):
        @pl.loop(0, charge.shape[1] // TILE)
        def _(step):
            span = pl.ds(pl.multiple_of(step * TILE, TILE), TILE)
            body(span, Stencil(cells, offs, span), charge[:, span])

    tz = (tz_h[...], tz_l[...])
    grid[...] = jnp.zeros_like(grid)

    def spread_core(span, near, amount):
        row_x = pick(near.x(), [w * amount for w in near.values(0)])
        row_y = pick(near.y(), near.values(1))
        planes = jnp.concatenate([row_x[x : x + 1] * row_y for x in range(CX)], axis=0)
        profile = halves(pick(near.z(), near.values(2)))
        rz_h[:, span], rz_l[:, span] = profile
        grid[core, :] += dot3(halves(planes), profile, NT)

    tiles(spread_core)
    ahead = [
        Exchange(pieces_x, src, dst, lanes, send_sem.at[k], recv_sem.at[k])
        for k, lanes in enumerate((core, edge))
    ]
    value = dot3(tz, halves(grid[core, :]), NT)
    pl.semaphore_wait(barrier, pieces - 1)
    ahead[0].put(value)

    def spread_edge(span, near, amount):
        heavy = [w * amount for w in near.values(0)]
        row_x = pick(near.x(), heavy)
        row_y = pick(near.y(), near.values(1))
        rim_x, rim_y = near.rim()
        rim = pick(rim_x, heavy) * pick(rim_y, near.values(1))
        planes = [row_x[x : x + 1] * row_y for x in range(CX, SPAN)] + [rim]
        planes = jnp.concatenate(planes, axis=0)
        grid[edge, :] += dot3(halves(planes), (rz_h[:, span], rz_l[:, span]), NT)

    tiles(spread_edge)
    ahead[1].put(dot3(tz, halves(grid[edge, :]), NT))

    def slopes_z(span, near, amount):
        dz_h[:, span], dz_l[:, span] = halves(pick(near.z(), near.slopes(2)))

    tiles(slopes_z)

    chunk = pieces_x * slice_z
    total_x = CX * pieces_x
    total_y = CY * pieces_y
    split = CX * chunk
    turned = grid

    def main_corners(planes):
        for x in planes:
            for j in range(pieces_y):
                lanes, own = pl.ds(x * chunk, chunk), pl.ds(j * chunk, chunk)
                yield (pl.ds(x * CY, CY), own), (pl.ds(j * CY, CY), lanes)

    def rim_corners():
        for x in range(SPAN):
            for j in range(pieces_y):
                lanes, own = pl.ds(x * chunk, chunk), pl.ds(j * chunk, chunk)
                yield (pl.ds(MAIN + x * RIM, RIM), own), (pl.ds(total_y + j * RIM, RIM), lanes)

    def edge_corners():
        yield from main_corners(range(CX, SPAN))
        yield from rim_corners()

    tails = pl.ds(split, wide.shape[1] - split)
    wide[:, tails] = jnp.zeros((wide.shape[0], wide.shape[1] - split), jnp.float32)
    ty = (ty_h[:, :total_y], ty_l[:, :total_y])
    ty_rim = (ty_h[:, total_y:], ty_l[:, total_y:])
    turned[core, :] = ahead[0].get().T
    for narrow, broad in main_corners(range(CX)):
        wide[broad] = turned[narrow]
    first = dot3(ty, halves(wide[:total_y, :split]), NN)
    turned[edge, :] = ahead[1].get().T
    for narrow, broad in edge_corners():
        wide[broad] = turned[narrow]
    last = dot3(ty, halves(wide[:total_y, split:]), NN)
    mixed = jnp.concatenate([first, last], axis=1) + dot3(ty_rim, halves(wide[total_y:, :]), NN)
    for load in loads:
        load.wait()
    mx = (mx_h[...], mx_l[...])
    spectrum = dot3(halves(mixed), mx, NN)
    width = spectrum.shape[1]

    def spread_scalar(ref, place):
        return jnp.full((1, width), ref[place], jnp.float32)

    s0, s1, s2 = (spread_scalar(spacing, d) for d in range(3))
    b = spread_scalar(beta, 0)
    squares = row1[...] / (s0 * s0) + row3[pl.ds(mine, 1), :] / (s2 * s2)
    squares = squares + col2[...] * (1.0 / (s1 * s1))
    safe = jnp.where(squares > 0.0, squares, 1.0)
    volume = s0 * s1 * s2 * float(total_x * total_y * NZ)
    table = jnp.exp(safe * (-(np.pi**2) / (b * b))) / (safe * (np.pi * volume))
    table = table * (rowm[pl.ds(mine, 1), :] * colm[...])
    spectrum = spectrum * jnp.where(squares > 0.0, table, 0.0)
    mixed = halves(dot3(halves(spectrum), mx, NT))
    after = [
        Exchange(pieces_x, back, home, lanes, send_sem.at[2 + k], recv_sem.at[2 + k])
        for k, lanes in enumerate((core, edge))
    ]
    wide[total_y:, :] = dot3(ty_rim, mixed, TN)
    wide[:total_y, split:] = dot3(ty, tuple(half[:, split:] for half in mixed), TN)
    turned[edge, :] = jnp.zeros((ROWS - CORE, NZ), jnp.float32)
    for narrow, broad in edge_corners():
        turned[narrow] = wide[broad]
    after[1].put(turned[edge, :].T)
    wide[:total_y, :split] = dot3(ty, tuple(half[:, :split] for half in mixed), TN)
    for narrow, broad in main_corners(range(CX)):
        turned[narrow] = wide[broad]
    after[0].put(turned[core, :].T)

    def fields(rows, span):
        def sampled_with(high, low):
            stacked = jnp.dot(
                window[: 2 * rows], high[:, span], preferred_element_type=jnp.float32
            )
            rest = jnp.dot(window[:rows], low[:, span], preferred_element_type=jnp.float32)
            return stacked[:rows] + (stacked[rows:] + rest)

        return sampled_with(rz_h, rz_l), sampled_with(dz_h, dz_l)

    def over_x(planes, rows, field):
        total = rows[planes[0] : planes[0] + 1] * field[0:CY]
        for k, x in enumerate(planes[1:], 1):
            total = total + rows[x : x + 1] * field[k * CY : (k + 1) * CY]
        return total

    def four_sums(planes, near, level, tilt):
        masks_x, masks_y = near.x(), near.y()
        row_x, tilt_x = pick(masks_x, near.values(0)), pick(masks_x, near.slopes(0))
        row_y, tilt_y = pick(masks_y, near.values(1)), pick(masks_y, near.slopes(1))
        plain = over_x(planes, row_x, level)
        return [
            jnp.sum(product, axis=0, keepdims=True)
            for product in (
                over_x(planes, tilt_x, level) * row_y,
                plain * tilt_y,
                over_x(planes, row_x, tilt) * row_y,
                plain * row_y,
            )
        ]

    def set_window(got):
        field = halves(dot3(halves(got.T), tz, NN))
        window[: 2 * got.shape[1]] = jnp.concatenate(field, axis=0)

    def gather_edge(span, near, amount):
        level, tilt = fields(ROWS - CORE, span)
        sums = four_sums(range(CX, SPAN), near, level, tilt)
        masks_x, masks_y = near.rim()
        row_x, tilt_x = pick(masks_x, near.values(0)), pick(masks_x, near.slopes(0))
        row_y, tilt_y = pick(masks_y, near.values(1)), pick(masks_y, near.slopes(1))
        level, tilt = level[MAIN - CORE :], tilt[MAIN - CORE :]
        flat = row_x * row_y
        extra = (level * tilt_x * row_y, level * row_x * tilt_y, tilt * flat, level * flat)
        for d in range(4):
            part[d, :, span] = sums[d] + jnp.sum(extra[d], axis=0, keepdims=True)

    set_window(after[1].get())
    tiles(gather_edge)

    def gather_core(span, near, amount):
        sums = four_sums(range(CX), near, *fields(CORE, span))
        for d in range(3):
            scale = jnp.full((1, TILE), spacing[d], jnp.float32)
            forces[d, :, span] = -amount * (sums[d] + part[d, :, span]) / scale
        energy[:, span] = 0.5 * amount * (sums[3] + part[3, :, span])

    set_window(after[0].get())
    tiles(gather_core)


def signed(length):
    index = np.arange(length)
    return np.where(2 * index < length, index, index - length)


def moduli(length):
    return 1.0 / ((2.0 + np.cos(2.0 * np.pi / length * np.arange(length))) / 3.0) ** 2


def middle_tables(pieces_x, pieces_y):
    pieces = pieces_x * pieces_y
    slice_z = NZ // pieces
    total_x, total_y = CX * pieces_x, CY * pieces_y
    rim = np.zeros((total_y, pieces_y, RIM))
    starts = CY * (np.arange(pieces_y) + 1)
    places = starts[:, None] + np.arange(RIM - 1)[None, :]
    rim[:, :, : RIM - 1] = cas(places.reshape(-1), total_y).reshape(total_y, pieces_y, RIM - 1)
    ty = np.concatenate([cas(np.arange(total_y), total_y), rim.reshape(total_y, -1)], axis=1)
    places = (np.arange(SPAN)[:, None] + CX * np.arange(pieces_x)[None, :]).reshape(-1)
    mx = np.kron(cas(places, total_x).T, np.eye(slice_z))
    depth = -(-mx.shape[0] // 128) * 128
    mx = np.concatenate([mx, np.zeros((depth - mx.shape[0], mx.shape[1]))], axis=0)
    row1 = np.repeat((signed(total_x) / total_x) ** 2, slice_z)[None, :]
    row3 = np.tile(((signed(NZ) / NZ) ** 2).reshape(pieces, slice_z), (1, total_x))
    rowm = np.tile(moduli(NZ).reshape(pieces, slice_z), (1, total_x))
    rowm = rowm * np.repeat(moduli(total_x), slice_z)[None, :]
    col2 = ((signed(total_y) / total_y) ** 2)[:, None]
    colm = moduli(total_y)[:, None]
    plain = tuple(jnp.asarray(t, jnp.float32) for t in (row1, row3, rowm, col2, colm))
    return constant_halves(ty) + constant_halves(mx) + plain


def local(base_cell, cell_offset, charges, spacing, ewald_beta):
    pieces_x = lax.axis_size("px")
    pieces_y = lax.axis_size("py")
    pieces = pieces_x * pieces_y
    charge = charges.reshape(1, -1)
    atoms = charge.shape[1]
    cells = jnp.transpose(base_cell, (0, 3, 1, 2)).reshape(3, 1, atoms)
    offs = jnp.transpose(cell_offset, (0, 3, 1, 2)).reshape(3, 1, atoms)
    tz = constant_halves(cas(np.arange(NZ), NZ))
    tables = middle_tables(pieces_x, pieces_y)
    vmem = pl.BlockSpec(memory_space=pltpu.VMEM)
    scalars = pl.BlockSpec(memory_space=pltpu.SMEM)
    anywhere = pl.BlockSpec(memory_space=pl.ANY)
    blocks = pltpu.VMEM((pieces, NZ // pieces, ROWS), jnp.float32)
    profile = pltpu.VMEM((NZ, atoms), jnp.bfloat16)
    forces, energy = pl.pallas_call(
        functools.partial(kernel, pieces_x, pieces_y),
        out_shape=(
            jax.ShapeDtypeStruct((3, 1, atoms), jnp.float32),
            jax.ShapeDtypeStruct((1, atoms), jnp.float32),
        ),
        in_specs=[vmem] * 3 + [scalars] * 2 + [vmem] * 4 + [anywhere] * 2 + [vmem] * 5,
        out_specs=(vmem, vmem),
        scratch_shapes=[
            pltpu.VMEM((ROWS, NZ), jnp.float32),
            pltpu.VMEM((tables[0].shape[1], tables[2].shape[0]), jnp.float32),
            pltpu.VMEM(tables[2].shape, jnp.bfloat16),
            pltpu.VMEM(tables[2].shape, jnp.bfloat16),
            profile,
            profile,
            profile,
            profile,
            pltpu.VMEM((2 * CORE, NZ), jnp.bfloat16),
            pltpu.VMEM((4, 1, atoms), jnp.float32),
            blocks,
            blocks,
            blocks,
            blocks,
            pltpu.SemaphoreType.DMA((2,)),
            pltpu.SemaphoreType.DMA((4, pieces)),
            pltpu.SemaphoreType.DMA((4, pieces)),
        ],
        compiler_params=pltpu.CompilerParams(
            vmem_limit_bytes=VMEM_LIMIT, collective_id=0, has_side_effects=True
        ),
        name="ewald",
    )(cells, offs, charge, spacing, ewald_beta, *tz, *tables)
    forces = jnp.transpose(forces.reshape(1, 3, 1, atoms), (0, 2, 3, 1))
    return forces, energy.reshape(charges.shape)


def solution(mesh):
    placed = (P("px", "py", None, None), P("px", "py", None, None), P("px", "py", None), P(), P())
    return jax.shard_map(
        local,
        mesh=mesh,
        in_specs=placed,
        out_specs=(P("px", "py", None, None), P("px", "py", None)),
        check_vma=False,
    )
```

time: 49 us -> 44.7 us (0.912)
  the two profiles are of different devices: /device:TPU:27 before, /device:TPU:0 now
where the time goes in v2:
time: 44.7 us; the launch traced here: 44.1 us
  Pallas kernels  40.7 us (91%)
  local copies, waits for them, and re-layouts  2.04 us (5%)
  between operations  1.29 us (3%)
    pallas_call x1, Pallas kernels, local(): pl.pallas_call(functools.partial(kernel, pieces_x, pieces_y), out_shape=(...  40.7 us
    unnamed x4, local copies, waits for them, and re-layouts  2.04 us

profile of v2, /device:TPU:0, one launch (start us, length us, event | category | flops | bytes accessed | tf_op | source)
XLA Modules:
  0.0 44.1 jit_solution(11165807081515557780)
XLA Ops:
  1.3 40.7 %ewald.1 = (f32[3,1,4096]{2,1,0:T(1,128)}, f32[1,4096]{1,0:T(1,128)}) custom-call(s32[3,1,4096]{2,1,0:T(1,128)} %bitcast.12, f32[3,1,4096]{2,1,0:T(1,128)} %bitcast.13, f32[1,4096]{1,0:T(1,128)} %bitcast.14, f32[3]{0:T(128)} %spacing.1, f32[1]{0:T(128)S(6)} %copy.20.beta, bf16[256,256]{1,0:T(8,128)(2,1)} %constant.22.clone.tz_h, ...), custom_call_target="tpu_custom_call" | custom-call | tf_op jit(solution)/shard_map/ewald/pallas_call | solution.py:400
  42.0 0.0 copy-start
  42.0 1.4 %copy.21 = f32[1,1,4096,3]{2,1,3,0:T(1,128)} copy(f32[1,1,4096,3]{2,1,3,0:T(1,128)} %bitcast.11) | data formatting | bytes 98304
  43.5 0.0 copy-done
  43.5 0.6 %copy.22 = f32[1,1,4096]{2,1,0:T(1,128)} copy(f32[1,1,4096]{2,1,0:T(1,128)S(1)} %bitcast.15) | data formatting | bytes 32768
Async XLA Ops:
  42.0 1.4 %copy-start = (f32[1,4096]{1,0:T(1,128)S(1)}, f32[1,4096]{1,0:T(1,128)}, u32[]{:S(2)}) copy-start(f32[1,4096]{1,0:T(1,128)} %get-tuple-element.5) | copy-start | bytes 49156

commit v3 on v2

--- a/solution.py
+++ b/solution.py
@@ -152,12 +152,14 @@
 def kernel(
     pieces_x, pieces_y, cells, offs, charge, spacing, beta, tz_h, tz_l, ty_h, ty_l, mx_hbm_h,
     mx_hbm_l, row1, row3, rowm, col2, colm, forces, energy, grid, wide, mx_h, mx_l, rz_h, rz_l,
-    dz_h, dz_l, window, part, src, dst, back, home, table_sem, send_sem, recv_sem,
+    dz_h, dz_l, window, part, weight, src, dst, back, home, table_sem, send_sem, recv_sem,
 ):
     pieces = pieces_x * pieces_y
     slice_z = NZ // pieces
     mine = lax.axis_index("py") * pieces_x + lax.axis_index("px")
-    core, edge = pl.ds(0, CORE), pl.ds(CORE, ROWS - CORE)
+    half = CX // 2
+    cores = [range(0, half), range(half, CX)]
+    rows_of = [pl.ds(k * half * CY, half * CY) for k in range(2)] + [pl.ds(CORE, ROWS - CORE)]
     loads = [
         pltpu.make_async_copy(mx_hbm_h, mx_h, table_sem.at[0]),
         pltpu.make_async_copy(mx_hbm_l, mx_l, table_sem.at[1]),
@@ -185,22 +187,11 @@
     tz = (tz_h[...], tz_l[...])
     grid[...] = jnp.zeros_like(grid)
 
-    def spread_core(span, near, amount):
-        row_x = pick(near.x(), [w * amount for w in near.values(0)])
-        row_y = pick(near.y(), near.values(1))
-        planes = jnp.concatenate([row_x[x : x + 1] * row_y for x in range(CX)], axis=0)
-        profile = halves(pick(near.z(), near.values(2)))
-        rz_h[:, span], rz_l[:, span] = profile
-        grid[core, :] += dot3(halves(planes), profile, NT)
-
-    tiles(spread_core)
-    ahead = [
-        Exchange(pieces_x, src, dst, lanes, send_sem.at[k], recv_sem.at[k])
-        for k, lanes in enumerate((core, edge))
-    ]
-    value = dot3(tz, halves(grid[core, :]), NT)
-    pl.semaphore_wait(barrier, pieces - 1)
-    ahead[0].put(value)
+    def exchanges(source, target, base):
+        return [
+            Exchange(pieces_x, source, target, rows, send_sem.at[base + k], recv_sem.at[base + k])
+            for k, rows in enumerate(rows_of)
+        ]
 
     def spread_edge(span, near, amount):
         heavy = [w * amount for w in near.values(0)]
@@ -209,11 +200,24 @@
         rim_x, rim_y = near.rim()
         rim = pick(rim_x, heavy) * pick(rim_y, near.values(1))
         planes = [row_x[x : x + 1] * row_y for x in range(CX, SPAN)] + [rim]
-        planes = jnp.concatenate(planes, axis=0)
-        grid[edge, :] += dot3(halves(planes), (rz_h[:, span], rz_l[:, span]), NT)
-
+        profile = halves(pick(near.z(), near.values(2)))
+        rz_h[:, span], rz_l[:, span] = profile
+        grid[rows_of[2], :] += dot3(halves(jnp.concatenate(planes, axis=0)), profile, NT)
+
+    def spread_core(k, span, near, amount):
+        row_x = pick(near.x(), [w * amount for w in near.values(0)])
+        row_y = pick(near.y(), near.values(1))
+        planes = jnp.concatenate([row_x[x : x + 1] * row_y for x in cores[k]], axis=0)
+        grid[rows_of[k], :] += dot3(halves(planes), (rz_h[:, span], rz_l[:, span]), NT)
+
+    ahead = exchanges(src, dst, 0)
     tiles(spread_edge)
-    ahead[1].put(dot3(tz, halves(grid[edge, :]), NT))
+    value = dot3(tz, halves(grid[rows_of[2], :]), NT)
+    pl.semaphore_wait(barrier, pieces - 1)
+    ahead[2].put(value)
+    for k in range(2):
+        tiles(functools.partial(spread_core, k))
+        ahead[k].put(dot3(tz, halves(grid[rows_of[k], :]), NT))
 
     def slopes_z(span, near, amount):
         dz_h[:, span], dz_l[:, span] = halves(pick(near.z(), near.slopes(2)))
@@ -246,20 +250,7 @@
     wide[:, tails] = jnp.zeros((wide.shape[0], wide.shape[1] - split), jnp.float32)
     ty = (ty_h[:, :total_y], ty_l[:, :total_y])
     ty_rim = (ty_h[:, total_y:], ty_l[:, total_y:])
-    turned[core, :] = ahead[0].get().T
-    for narrow, broad in main_corners(range(CX)):
-        wide[broad] = turned[narrow]
-    first = dot3(ty, halves(wide[:total_y, :split]), NN)
-    turned[edge, :] = ahead[1].get().T
-    for narrow, broad in edge_corners():
-        wide[broad] = turned[narrow]
-    last = dot3(ty, halves(wide[:total_y, split:]), NN)
-    mixed = jnp.concatenate([first, last], axis=1) + dot3(ty_rim, halves(wide[total_y:, :]), NN)
-    for load in loads:
-        load.wait()
-    mx = (mx_h[...], mx_l[...])
-    spectrum = dot3(halves(mixed), mx, NN)
-    width = spectrum.shape[1]
+    width = mx_h.shape[1]
 
     def spread_scalar(ref, place):
         return jnp.full((1, width), ref[place], jnp.float32)
@@ -272,22 +263,41 @@
     volume = s0 * s1 * s2 * float(total_x * total_y * NZ)
     table = jnp.exp(safe * (-(np.pi**2) / (b * b))) / (safe * (np.pi * volume))
     table = table * (rowm[pl.ds(mine, 1), :] * colm[...])
-    spectrum = spectrum * jnp.where(squares > 0.0, table, 0.0)
-    mixed = halves(dot3(halves(spectrum), mx, NT))
-    after = [
-        Exchange(pieces_x, back, home, lanes, send_sem.at[2 + k], recv_sem.at[2 + k])
-        for k, lanes in enumerate((core, edge))
-    ]
-    wide[total_y:, :] = dot3(ty_rim, mixed, TN)
-    wide[:total_y, split:] = dot3(ty, tuple(half[:, split:] for half in mixed), TN)
-    turned[edge, :] = jnp.zeros((ROWS - CORE, NZ), jnp.float32)
+    weight[...] = jnp.where(squares > 0.0, table, 0.0)
+    for load in loads:
+        load.wait()
+
+    turned[rows_of[2], :] = ahead[2].get().T
+    for narrow, broad in edge_corners():
+        wide[broad] = turned[narrow]
+    mixed = dot3(ty_rim, halves(wide[total_y:, :]), NN)
+    last = dot3(ty, halves(wide[:total_y, split:]), NN)
+    mixed = jnp.concatenate([mixed[:, :split], mixed[:, split:] + last], axis=1)
+    spectrum = dot3(halves(mixed), (mx_h[...], mx_l[...]), NN)
+    strips = [pl.ds(k * half * chunk, half * chunk) for k in range(2)]
+    for k in range(2):
+        turned[rows_of[k], :] = ahead[k].get().T
+        for narrow, broad in main_corners(cores[k]):
+            wide[broad] = turned[narrow]
+        mixed = dot3(ty, halves(wide[:total_y, strips[k]]), NN)
+        spectrum = spectrum + dot3(halves(mixed), (mx_h[strips[k], :], mx_l[strips[k], :]), NN)
+    spectrum = halves(spectrum * weight[...])
+    after = exchanges(back, home, 3)
+    mixed = []
+    for k in range(2):
+        mixed.append(halves(dot3(spectrum, (mx_h[strips[k], :], mx_l[strips[k], :]), NT)))
+        wide[:total_y, strips[k]] = dot3(ty, mixed[k], TN)
+        for narrow, broad in main_corners(cores[k]):
+            turned[narrow] = wide[broad]
+        after[k].put(turned[rows_of[k], :].T)
+    mixed.append(halves(dot3(spectrum, (mx_h[tails, :], mx_l[tails, :]), NT)))
+    wide[:total_y, split:] = dot3(ty, mixed[2], TN)
+    joined = tuple(jnp.concatenate(group, axis=1) for group in zip(*mixed))
+    wide[total_y:, :] = dot3(ty_rim, joined, TN)
+    turned[rows_of[2], :] = jnp.zeros((ROWS - CORE, NZ), jnp.float32)
     for narrow, broad in edge_corners():
         turned[narrow] = wide[broad]
-    after[1].put(turned[edge, :].T)
-    wide[:total_y, :split] = dot3(ty, tuple(half[:, :split] for half in mixed), TN)
-    for narrow, broad in main_corners(range(CX)):
-        turned[narrow] = wide[broad]
-    after[0].put(turned[core, :].T)
+    after[2].put(turned[rows_of[2], :].T)
 
     def fields(rows, span):
         def sampled_with(high, low):
@@ -324,6 +334,15 @@
         field = halves(dot3(halves(got.T), tz, NN))
         window[: 2 * got.shape[1]] = jnp.concatenate(field, axis=0)
 
+    def gather_core(k, span, near, amount):
+        sums = four_sums(cores[k], near, *fields(half * CY, span))
+        for d in range(4):
+            part[d, :, span] = sums[d] + part[d, :, span] if k else sums[d]
+
+    for k in range(2):
+        set_window(after[k].get())
+        tiles(functools.partial(gather_core, k))
+
     def gather_edge(span, near, amount):
         level, tilt = fields(ROWS - CORE, span)
         sums = four_sums(range(CX, SPAN), near, level, tilt)
@@ -333,21 +352,17 @@
         level, tilt = level[MAIN - CORE :], tilt[MAIN - CORE :]
         flat = row_x * row_y
         extra = (level * tilt_x * row_y, level * row_x * tilt_y, tilt * flat, level * flat)
-        for d in range(4):
-            part[d, :, span] = sums[d] + jnp.sum(extra[d], axis=0, keepdims=True)
-
-    set_window(after[1].get())
-    tiles(gather_edge)
-
-    def gather_core(span, near, amount):
-        sums = four_sums(range(CX), near, *fields(CORE, span))
+        sums = [
+            sums[d] + (jnp.sum(extra[d], axis=0, keepdims=True) + part[d, :, span])
+            for d in range(4)
+        ]
         for d in range(3):
             scale = jnp.full((1, TILE), spacing[d], jnp.float32)
-            forces[d, :, span] = -amount * (sums[d] + part[d, :, span]) / scale
-        energy[:, span] = 0.5 * amount * (sums[3] + part[3, :, span])
-
-    set_window(after[0].get())
-    tiles(gather_core)
+            forces[d, :, span] = -amount * sums[d] / scale
+        energy[:, span] = 0.5 * amount * sums[3]
+
+    set_window(after[2].get())
+    tiles(gather_edge)
 
 
 def signed(length):
@@ -414,15 +429,16 @@
             profile,
             profile,
             profile,
-            pltpu.VMEM((2 * CORE, NZ), jnp.bfloat16),
+            pltpu.VMEM((CORE, NZ), jnp.bfloat16),
             pltpu.VMEM((4, 1, atoms), jnp.float32),
+            pltpu.VMEM((tables[0].shape[0], tables[2].shape[1]), jnp.float32),
             blocks,
             blocks,
             blocks,
             blocks,
             pltpu.SemaphoreType.DMA((2,)),
-            pltpu.SemaphoreType.DMA((4, pieces)),
-            pltpu.SemaphoreType.DMA((4, pieces)),
+            pltpu.SemaphoreType.DMA((6, pieces)),
+            pltpu.SemaphoreType.DMA((6, pieces)),
         ],
         compiler_params=pltpu.CompilerParams(
             vmem_limit_bytes=VMEM_LIMIT, collective_id=0, has_side_effects=True

time: 44.7 us -> 50.1 us (1.12)
  Pallas kernels: 40.7 us -> 46.1 us
    pallas_call x1, Pallas kernels: 40.7 us -> 46.1 us  [local(): pl.pallas_call(functools.partial(kernel, pieces_x, pieces_y), out_shape=(...]
where the time goes in v3:
time: 50.1 us; the launch traced here: 49.5 us
  Pallas kernels  46.1 us (92%)
  local copies, waits for them, and re-layouts  2.04 us (4%)
  between operations  1.29 us (3%)
    pallas_call x1, Pallas kernels, local(): pl.pallas_call(functools.partial(kernel, pieces_x, pieces_y), out_shape=(...  46.1 us
    unnamed x4, local copies, waits for them, and re-layouts  2.04 us

profile of v3, /device:TPU:0, one launch (start us, length us, event | category | flops | bytes accessed | tf_op | source)
XLA Modules:
  0.0 49.5 jit_solution(10059345386377225654)
XLA Ops:
  1.3 46.1 %ewald.1 = (f32[3,1,4096]{2,1,0:T(1,128)}, f32[1,4096]{1,0:T(1,128)}) custom-call(s32[3,1,4096]{2,1,0:T(1,128)} %bitcast.12, f32[3,1,4096]{2,1,0:T(1,128)} %bitcast.13, f32[1,4096]{1,0:T(1,128)} %bitcast.14, f32[3]{0:T(128)} %spacing.1, f32[1]{0:T(128)S(6)} %copy.20.beta, bf16[256,256]{1,0:T(8,128)(2,1)} %constant.22.clone.tz_h, ...), custom_call_target="tpu_custom_call" | custom-call | tf_op jit(solution)/shard_map/ewald/pallas_call | solution.py:415
  47.4 0.0 copy-start
  47.4 1.4 %copy.21 = f32[1,1,4096,3]{2,1,3,0:T(1,128)} copy(f32[1,1,4096,3]{2,1,3,0:T(1,128)} %bitcast.11) | data formatting | bytes 98304
  48.8 0.0 copy-done
  48.9 0.6 %copy.22 = f32[1,1,4096]{2,1,0:T(1,128)} copy(f32[1,1,4096]{2,1,0:T(1,128)S(1)} %bitcast.15) | data formatting | bytes 32768
Async XLA Ops:
  47.4 1.4 %copy-start = (f32[1,4096]{1,0:T(1,128)S(1)}, f32[1,4096]{1,0:T(1,128)}, u32[]{:S(2)}) copy-start(f32[1,4096]{1,0:T(1,128)} %get-tuple-element.5) | copy-start | bytes 49156

commit v4 on v2

--- a/solution.py
+++ b/solution.py
@@ -121,13 +121,13 @@
         self.pieces = src.shape[0]
         self.mine = lax.axis_index("py") * pieces_x + lax.axis_index("px")
 
-    def copy(self, step):
+    def copy(self, step, here, there):
         peer = (self.mine + step) % self.pieces
         return pltpu.make_async_remote_copy(
-            src_ref=self.src.at[peer, :, self.lanes],
-            dst_ref=self.dst.at[self.mine, :, self.lanes],
-            send_sem=self.send_sem.at[step],
-            recv_sem=self.recv_sem.at[step],
+            src_ref=self.src.at[peer if here is None else here, :, self.lanes],
+            dst_ref=self.dst.at[there, :, self.lanes],
+            send_sem=self.send_sem,
+            recv_sem=self.recv_sem,
             device_id=(peer % self.pieces_x, peer // self.pieces_x),
             device_id_type=pl.DeviceIdType.MESH,
         )
@@ -135,24 +135,21 @@
     def put(self, value):
         self.src[:, :, self.lanes] = value.reshape(self.src.shape[:2] + (value.shape[1],))
 
-        @pl.loop(1, self.pieces)
-        def _(step):
-            self.copy(step).start()
+        for step in range(1, self.pieces):
+            self.copy(step, None, self.mine).start()
 
         self.dst[self.mine, :, self.lanes] = self.src[self.mine, :, self.lanes]
 
     def get(self):
-        @pl.loop(1, self.pieces)
-        def _(step):
-            self.copy(step).wait()
-
+        every = pl.ds(0, self.pieces - 1)
+        self.copy(1, every, every).wait()
         return self.dst[:, :, self.lanes].reshape(NZ, -1)
 
 
 def kernel(
     pieces_x, pieces_y, cells, offs, charge, spacing, beta, tz_h, tz_l, ty_h, ty_l, mx_hbm_h,
     mx_hbm_l, row1, row3, rowm, col2, colm, forces, energy, grid, wide, mx_h, mx_l, rz_h, rz_l,
-    dz_h, dz_l, window, part, src, dst, back, home, table_sem, send_sem, recv_sem,
+    dz_h, dz_l, window, part, weight, src, dst, back, home, table_sem, send_sem, recv_sem,
 ):
     pieces = pieces_x * pieces_y
     slice_z = NZ // pieces
@@ -246,6 +243,22 @@
     wide[:, tails] = jnp.zeros((wide.shape[0], wide.shape[1] - split), jnp.float32)
     ty = (ty_h[:, :total_y], ty_l[:, :total_y])
     ty_rim = (ty_h[:, total_y:], ty_l[:, total_y:])
+    width = mx_h.shape[1]
+
+    def spread_scalar(ref, place):
+        return jnp.full((1, width), ref[place], jnp.float32)
+
+    s0, s1, s2 = (spread_scalar(spacing, d) for d in range(3))
+    b = spread_scalar(beta, 0)
+    squares = row1[...] / (s0 * s0) + row3[pl.ds(mine, 1), :] / (s2 * s2)
+    squares = squares + col2[...] * (1.0 / (s1 * s1))
+    safe = jnp.where(squares > 0.0, squares, 1.0)
+    volume = s0 * s1 * s2 * float(total_x * total_y * NZ)
+    table = jnp.exp(safe * (-(np.pi**2) / (b * b))) / (safe * (np.pi * volume))
+    table = table * (rowm[pl.ds(mine, 1), :] * colm[...])
+    weight[...] = jnp.where(squares > 0.0, table, 0.0)
+    for load in loads:
+        load.wait()
     turned[core, :] = ahead[0].get().T
     for narrow, broad in main_corners(range(CX)):
         wide[broad] = turned[narrow]
@@ -255,24 +268,9 @@
         wide[broad] = turned[narrow]
     last = dot3(ty, halves(wide[:total_y, split:]), NN)
     mixed = jnp.concatenate([first, last], axis=1) + dot3(ty_rim, halves(wide[total_y:, :]), NN)
-    for load in loads:
-        load.wait()
     mx = (mx_h[...], mx_l[...])
     spectrum = dot3(halves(mixed), mx, NN)
-    width = spectrum.shape[1]
-
-    def spread_scalar(ref, place):
-        return jnp.full((1, width), ref[place], jnp.float32)
-
-    s0, s1, s2 = (spread_scalar(spacing, d) for d in range(3))
-    b = spread_scalar(beta, 0)
-    squares = row1[...] / (s0 * s0) + row3[pl.ds(mine, 1), :] / (s2 * s2)
-    squares = squares + col2[...] * (1.0 / (s1 * s1))
-    safe = jnp.where(squares > 0.0, squares, 1.0)
-    volume = s0 * s1 * s2 * float(total_x * total_y * NZ)
-    table = jnp.exp(safe * (-(np.pi**2) / (b * b))) / (safe * (np.pi * volume))
-    table = table * (rowm[pl.ds(mine, 1), :] * colm[...])
-    spectrum = spectrum * jnp.where(squares > 0.0, table, 0.0)
+    spectrum = spectrum * weight[...]
     mixed = halves(dot3(halves(spectrum), mx, NT))
     after = [
         Exchange(pieces_x, back, home, lanes, send_sem.at[2 + k], recv_sem.at[2 + k])
@@ -416,13 +414,14 @@
             profile,
             pltpu.VMEM((2 * CORE, NZ), jnp.bfloat16),
             pltpu.VMEM((4, 1, atoms), jnp.float32),
+            pltpu.VMEM((tables[0].shape[0], tables[2].shape[1]), jnp.float32),
             blocks,
             blocks,
             blocks,
             blocks,
             pltpu.SemaphoreType.DMA((2,)),
-            pltpu.SemaphoreType.DMA((4, pieces)),
-            pltpu.SemaphoreType.DMA((4, pieces)),
+            pltpu.SemaphoreType.DMA((4,)),
+            pltpu.SemaphoreType.DMA((4,)),
         ],
         compiler_params=pltpu.CompilerParams(
             vmem_limit_bytes=VMEM_LIMIT, collective_id=0, has_side_effects=True

time: 44.7 us -> 42.3 us (0.946)
  Pallas kernels: 40.7 us -> 38.2 us
    pallas_call x1, Pallas kernels: 40.7 us -> 38.2 us  [local(): pl.pallas_call(functools.partial(kernel, pieces_x, pieces_y), out_shape=(...]
where the time goes in v4:
time: 42.3 us; the launch traced here: 41.5 us
  Pallas kernels  38.2 us (90%)
  local copies, waits for them, and re-layouts  2.04 us (5%)
  between operations  1.29 us (3%)
    pallas_call x1, Pallas kernels, local(): pl.pallas_call(functools.partial(kernel, pieces_x, pieces_y), out_shape=(...  38.2 us
    unnamed x4, local copies, waits for them, and re-layouts  2.04 us

profile of v4, /device:TPU:0, one launch (start us, length us, event | category | flops | bytes accessed | tf_op | source)
XLA Modules:
  0.0 41.5 jit_solution(8546902522571001749)
XLA Ops:
  1.3 38.2 %ewald.1 = (f32[3,1,4096]{2,1,0:T(1,128)}, f32[1,4096]{1,0:T(1,128)}) custom-call(s32[3,1,4096]{2,1,0:T(1,128)} %bitcast.12, f32[3,1,4096]{2,1,0:T(1,128)} %bitcast.13, f32[1,4096]{1,0:T(1,128)} %bitcast.14, f32[3]{0:T(128)} %spacing.1, f32[1]{0:T(128)S(6)} %copy.20.beta, bf16[256,256]{1,0:T(8,128)(2,1)} %constant.22.clone.tz_h, ...), custom_call_target="tpu_custom_call" | custom-call | tf_op jit(solution)/shard_map/ewald/pallas_call | solution.py:398
  39.5 0.0 copy-start
  39.5 1.4 %copy.21 = f32[1,1,4096,3]{2,1,3,0:T(1,128)} copy(f32[1,1,4096,3]{2,1,3,0:T(1,128)} %bitcast.11) | data formatting | bytes 98304
  40.9 0.0 copy-done
  40.9 0.6 %copy.22 = f32[1,1,4096]{2,1,0:T(1,128)} copy(f32[1,1,4096]{2,1,0:T(1,128)S(1)} %bitcast.15) | data formatting | bytes 32768
Async XLA Ops:
  39.5 1.4 %copy-start = (f32[1,4096]{1,0:T(1,128)S(1)}, f32[1,4096]{1,0:T(1,128)}, u32[]{:S(2)}) copy-start(f32[1,4096]{1,0:T(1,128)} %get-tuple-element.5) | copy-start | bytes 49156

commit v5 on v4

--- a/solution.py
+++ b/solution.py
@@ -17,6 +17,7 @@
 CORE = CX * CY
 ROWS = -(-(MAIN + SPAN * RIM) // 128) * 128
 TILE = 512
+TWIN = 2
 VMEM_LIMIT = 60 * 1024 * 1024
 NN = (((1,), (0,)), ((), ()))
 NT = (((1,), (1,)), ((), ()))
@@ -163,8 +164,7 @@
         load.start()
     barrier = pltpu.get_barrier_semaphore()
 
-    @pl.loop(1, pieces)
-    def _(step):
+    for step in range(1, pieces):
         peer = (mine + step) % pieces
         pl.semaphore_signal(
             barrier,
@@ -174,10 +174,11 @@
         )
 
     def tiles(body):
-        @pl.loop(0, charge.shape[1] // TILE)
+        @pl.loop(0, charge.shape[1] // (TILE * TWIN))
         def _(step):
-            span = pl.ds(pl.multiple_of(step * TILE, TILE), TILE)
-            body(span, Stencil(cells, offs, span), charge[:, span])
+            for twin in range(TWIN):
+                span = pl.ds(pl.multiple_of((step * TWIN + twin) * TILE, TILE), TILE)
+                body(span, Stencil(cells, offs, span), charge[:, span])
 
     tz = (tz_h[...], tz_l[...])
     grid[...] = jnp.zeros_like(grid)

time: 42.3 us -> 40.8 us (0.965)
  the two profiles are of different devices: /device:TPU:0 before, /device:TPU:15 now
where the time goes in v5:
time: 40.8 us; the launch traced here: 40.5 us
  Pallas kernels  37.2 us (91%)
  local copies, waits for them, and re-layouts  2.04 us (5%)
  between operations  1.29 us (3%)
    pallas_call x1, Pallas kernels, local(): pl.pallas_call(functools.partial(kernel, pieces_x, pieces_y), out_shape=(...  37.2 us
    unnamed x4, local copies, waits for them, and re-layouts  2.04 us

profile of v5, /device:TPU:15, one launch (start us, length us, event | category | flops | bytes accessed | tf_op | source)
XLA Modules:
  0.0 40.5 jit_solution(17328143050229636011)
XLA Ops:
  1.3 37.2 %ewald.1 = (f32[3,1,4096]{2,1,0:T(1,128)}, f32[1,4096]{1,0:T(1,128)}) custom-call(s32[3,1,4096]{2,1,0:T(1,128)} %bitcast.12, f32[3,1,4096]{2,1,0:T(1,128)} %bitcast.13, f32[1,4096]{1,0:T(1,128)} %bitcast.14, f32[3]{0:T(128)} %spacing.1, f32[1]{0:T(128)S(6)} %copy.20.beta, bf16[256,256]{1,0:T(8,128)(2,1)} %constant.22.clone.tz_h, ...), custom_call_target="tpu_custom_call" | custom-call | tf_op jit(solution)/shard_map/ewald/pallas_call | solution.py:399
  38.5 0.0 copy-start
  38.5 1.4 %copy.21 = f32[1,1,4096,3]{2,1,3,0:T(1,128)} copy(f32[1,1,4096,3]{2,1,3,0:T(1,128)} %bitcast.11) | data formatting | bytes 98304
  39.9 0.0 copy-done
  39.9 0.6 %copy.22 = f32[1,1,4096]{2,1,0:T(1,128)} copy(f32[1,1,4096]{2,1,0:T(1,128)S(1)} %bitcast.15) | data formatting | bytes 32768
Async XLA Ops:
  38.5 1.4 %copy-start = (f32[1,4096]{1,0:T(1,128)S(1)}, f32[1,4096]{1,0:T(1,128)}, u32[]{:S(2)}) copy-start(f32[1,4096]{1,0:T(1,128)} %get-tuple-element.5) | copy-start | bytes 49156

commit v6 on v5

--- a/solution.py
+++ b/solution.py
@@ -17,7 +17,7 @@
 CORE = CX * CY
 ROWS = -(-(MAIN + SPAN * RIM) // 128) * 128
 TILE = 512
-TWIN = 2
+TWIN = 4
 VMEM_LIMIT = 60 * 1024 * 1024
 NN = (((1,), (0,)), ((), ()))
 NT = (((1,), (1,)), ((), ()))

time: 40.8 us -> 39.9 us (0.978)
  the two profiles are of different devices: /device:TPU:15 before, /device:TPU:0 now
where the time goes in v6:
time: 39.9 us; the launch traced here: 39.1 us
  Pallas kernels  35.8 us (90%)
  local copies, waits for them, and re-layouts  2.04 us (5%)
  between operations  1.29 us (3%)
    pallas_call x1, Pallas kernels, local(): pl.pallas_call(functools.partial(kernel, pieces_x, pieces_y), out_shape=(...  35.8 us
    unnamed x4, local copies, waits for them, and re-layouts  2.04 us

profile of v6, /device:TPU:0, one launch (start us, length us, event | category | flops | bytes accessed | tf_op | source)
XLA Modules:
  0.0 39.1 jit_solution(11948059608497007322)
XLA Ops:
  1.3 35.8 %ewald.1 = (f32[3,1,4096]{2,1,0:T(1,128)}, f32[1,4096]{1,0:T(1,128)}) custom-call(s32[3,1,4096]{2,1,0:T(1,128)} %bitcast.12, f32[3,1,4096]{2,1,0:T(1,128)} %bitcast.13, f32[1,4096]{1,0:T(1,128)} %bitcast.14, f32[3]{0:T(128)} %spacing.1, f32[1]{0:T(128)S(6)} %copy.20.beta, bf16[256,256]{1,0:T(8,128)(2,1)} %constant.22.clone.tz_h, ...), custom_call_target="tpu_custom_call" | custom-call | tf_op jit(solution)/shard_map/ewald/pallas_call | solution.py:399
  37.0 0.0 copy-start
  37.1 1.4 %copy.21 = f32[1,1,4096,3]{2,1,3,0:T(1,128)} copy(f32[1,1,4096,3]{2,1,3,0:T(1,128)} %bitcast.11) | data formatting | bytes 98304
  38.5 0.0 copy-done
  38.5 0.6 %copy.22 = f32[1,1,4096]{2,1,0:T(1,128)} copy(f32[1,1,4096]{2,1,0:T(1,128)S(1)} %bitcast.15) | data formatting | bytes 32768
Async XLA Ops:
  37.0 1.4 %copy-start = (f32[1,4096]{1,0:T(1,128)S(1)}, f32[1,4096]{1,0:T(1,128)}, u32[]{:S(2)}) copy-start(f32[1,4096]{1,0:T(1,128)} %get-tuple-element.5) | copy-start | bytes 49156
